TPU v7x, 32 devices: a whole 2x2x4 slice. The times are simulated.
32 devices in a mesh: rows: 8 (over z, y), protos: 4 (over x, core).
Axes of the slice: x: 2, y: 2, z: 4, core: 2. Of those that a mesh axis runs over, the one named last changes fastest.
Arguments:
- features: bfloat16 [3072, 256], P('rows', 'protos'), may hold values from -12 to 12
- prototypes: bfloat16 [65536, 256], P('protos', 'rows'), may hold values from -8 to 8
- masked_index: int32 [1536], P('rows'), may hold values from 0 to 383
Outputs:
- targets: bfloat16 [1536, 65536], P('rows', 'protos')
Inputs may be any that keep to these rules, and one draw needn't show every extreme that they name: Row r of the whole takes patch (r // 192) * 384 + masked_index[r] of features.
All inputs are finite; a program needn't handle non-finite values.
Results may differ from a plain program's by a relative error of at most 0.001.
Values may be sent and summed in bfloat16 or wider, within the bound.
A program may use at most 64 MiB of HBM per device.

v0:
```python
import jax
import jax.numpy as jnp
from jax import lax
from jax.sharding import PartitionSpec as P

K = 65536
ITERS = 3
TEMP = 0.07
EPS = 1e-06


def on_device(features, prototypes, masked_index):
    chosen = jnp.take(features, masked_index, axis=0)
    patches = lax.all_gather(chosen, "protos", axis=1, tiled=True)
    feat_scale = lax.rsqrt(jnp.sum(jnp.square(patches.astype(jnp.float32)), axis=1) + EPS)
    full = lax.all_gather(prototypes, "rows", axis=1, tiled=True)
    proto_sq = jnp.sum(jnp.square(full.astype(jnp.float32)), axis=1)
    raw = lax.dot_general(
        patches, full, (((1,), (1,)), ((), ())), preferred_element_type=jnp.float32
    )
    proto_scale = lax.rsqrt(proto_sq + EPS)
    weights = jnp.exp(raw * feat_scale[:, None] * proto_scale[None, :] / TEMP)
    total_rows = masked_index.shape[0] * lax.axis_size("rows")
    row_scale = jnp.ones((patches.shape[0],), jnp.float32)
    for step in range(ITERS):
        col_part = jnp.dot(row_scale, weights, precision=lax.Precision.HIGHEST)
        col_scale = 1.0 / (K * lax.psum(col_part, "rows"))
        row_part = jnp.dot(weights, col_scale, precision=lax.Precision.HIGHEST)
        row_scale = 1.0 / (total_rows * lax.psum(row_part, "protos"))
    factor = float(K) * float(total_rows)
    return (factor * row_scale[:, None] * weights * col_scale[None, :]).astype(jnp.bfloat16)


def solution(mesh):
    in_specs = (P("rows", "protos"), P("protos", "rows"), P("rows"))
    out_specs = P("rows", "protos")
    return jax.shard_map(
        on_device, mesh=mesh, in_specs=in_specs, out_specs=out_specs, check_vma=False
    )
```

profile of v0, /device:TPU:0, one launch (start us, length us, event | category | flops | bytes accessed | tf_op | source)
XLA Modules:
  0.0 458.1 jit_solution(18258766225013638009)
XLA Ops:
  6.5 0.7 all-gather.2.cloned.1.call-update
  7.3 0.0 all-reduce.4.cloned.1.call-start
  7.3 0.9 copy.5
  8.2 0.7 compare_select_fusion
  8.9 0.8 gather_fusion
  9.7 0.7 compare_and_fusion
  10.4 0.1 broadcast_select_fusion
  10.5 0.1 copy.6
  10.6 6.5 %all_gather.6 = bf16[192,256]{0,1:T(8,128)(2,1)S(1)} all-gather(bf16[192,64]{0,1:T(8,128)(2,1)S(1)} %copy.6), channel_id=1, replica_groups=mesh['rows'=8,'protos'=4] {'protos'}, dimensions={1}, use_global_device_ids=true | all-gather | bytes 122880 | tf_op jit(solution)/shard_map/all_gather | solution.py:14
  17.1 0.1 multiply_reduce_fusion.1
  17.2 119.5 %all-gather.2.cloned.1.call-done = bf16[16384,256]{0,1:T(8,128)(2,1)} async-done(((bf16[16384,32]{0,1:T(8,128)(2,1)}), bf16[16384,256]{0,1:T(8,128)(2,1)}) %all-gather.2.cloned.1.call-update) | async-done | bytes 8388624 | tf_op jit(solution)/shard_map/all_gather | solution.py:16
  136.7 5.1 %multiply_reduce_fusion = f32[16384]{0:T(1024)S(1)} fusion(bf16[16384,256]{0,1:T(8,128)(2,1)} %all-gather.2.cloned.1.call-done), kind=kLoop, calls=%fused_computation.5 | loop fusion | flops 12566528 | bytes 8454144 | tf_op jit(solution)/shard_map/reduce_sum | solution.py:17
  141.8 5.8 %fusion.2 = f32[192,16384]{1,0:T(8,128)S(1)} fusion(bf16[192,256]{0,1:T(8,128)(2,1)S(1)} %all_gather.6, bf16[16384,256]{0,1:T(8,128)(2,1)} %all-gather.2.cloned.1.call-done, f32[16384]{0:T(1024)S(1)} %add_rsqrt_fusion, f32[192]{0:T(256)S(1)} %add_rsqrt_fusion.1), kind=kOutput, calls=%fused_computation.4 | convolution fusion | flops 1620049920 | bytes 21136128 | tf_op jit(solution)/shard_map/dot_general | solution.py:18
  147.7 4.6 copy-done
  152.2 6.6 %fusion.3 = f32[1,16384]{1,0:T(1,128)} fusion(f32[192,16384]{1,0:T(8,128)S(1)} %fusion.2), kind=kOutput, calls=%fused_computation.20 | convolution fusion | flops 37748736 | bytes 12648448 | tf_op jit(solution)/shard_map/dot_general | solution.py:26
  158.9 0.2 all-reduce.6.cloned.1.call-start
  159.1 67.3 %all-reduce.4.cloned.1.call-done = f32[16384]{0:T(1024)} async-done(((f32[16384]{0:T(1024)}), f32[16384]{0:T(1024)}) %all-reduce.4.cloned.1.call-update) | async-done | bytes 65552 | tf_op jit(solution)/shard_map/psum | solution.py:27
  226.4 0.9 multiply_divide_fusion.2
  227.3 12.7 %fusion.6 = f32[1,192]{1,0:T(1,128)S(1)} fusion(f32[192,16384]{1,0:T(8,128)} %copy-done, f32[16384,1]{0,1:T(1,128)S(1)} %bitcast.28), kind=kOutput, calls=%fused_computation.23 | convolution fusion | flops 37748736 | bytes 12649216 | tf_op jit(solution)/shard_map/dot_general | solution.py:28
  240.0 5.7 %psum.43 = f32[192]{0:T(256)S(1)} all-reduce(f32[192]{0:T(256)S(1)} %bitcast.30), channel_id=1, replica_groups=mesh['rows'=8,'protos'=4] {'protos'}, use_global_device_ids=true, to_apply=%region_3.4 | all-reduce | flops 192 | bytes 1536 | tf_op jit(solution)/shard_map/psum | solution.py:29
  245.7 9.5 %fusion.7 = f32[1,16384]{1,0:T(1,128)} fusion(f32[192,1]{0,1:T(1,128)S(1)} %bitcast.31, f32[192,16384]{1,0:T(8,128)} %copy-done), kind=kOutput, calls=%fused_computation.24 | convolution fusion | flops 37748736 | bytes 12649216 | tf_op jit(solution)/shard_map/dot_general | solution.py:26
  255.2 0.0 all-reduce.8.cloned.1.call-start
  255.3 69.6 %all-reduce.6.cloned.1.call-done = f32[16384]{0:T(1024)} async-done(((f32[16384]{0:T(1024)}), f32[16384]{0:T(1024)}) %all-reduce.6.cloned.1.call-update) | async-done | bytes 65552 | tf_op jit(solution)/shard_map/psum | solution.py:27
  324.8 0.9 multiply_divide_fusion.1
  325.7 12.7 %fusion.8 = f32[1,192]{1,0:T(1,128)S(1)} fusion(f32[192,16384]{1,0:T(8,128)} %copy-done, f32[16384,1]{0,1:T(1,128)S(1)} %bitcast.29), kind=kOutput, calls=%fused_computation.25 | convolution fusion | flops 37748736 | bytes 12649216 | tf_op jit(solution)/shard_map/dot_general | solution.py:28
  338.4 5.9 %psum.45 = f32[192]{0:T(256)S(1)} all-reduce(f32[192]{0:T(256)S(1)} %bitcast.32), channel_id=1, replica_groups=mesh['rows'=8,'protos'=4] {'protos'}, use_global_device_ids=true, to_apply=%region_5.6 | all-reduce | flops 192 | bytes 1536 | tf_op jit(solution)/shard_map/psum | solution.py:29
  344.3 9.5 %fusion.9 = f32[1,16384]{1,0:T(1,128)} fusion(f32[192,1]{0,1:T(1,128)S(1)} %bitcast.33, f32[192,16384]{1,0:T(8,128)} %copy-done), kind=kOutput, calls=%fused_computation.26 | convolution fusion | flops 37748736 | bytes 12649216 | tf_op jit(solution)/shard_map/dot_general | solution.py:26
  353.8 69.6 %all-reduce.8.cloned.1.call-done = f32[16384]{0:T(1024)} async-done(((f32[16384]{0:T(1024)}), f32[16384]{0:T(1024)}) %all-reduce.8.cloned.1.call-update) | async-done | bytes 65552 | tf_op jit(solution)/shard_map/psum | solution.py:27
  423.5 0.9 multiply_divide_fusion
  424.3 12.7 %fusion.10 = f32[1,192]{1,0:T(1,128)S(1)} fusion(f32[192,16384]{1,0:T(8,128)} %copy-done, f32[16384,1]{0,1:T(1,128)S(1)} %bitcast.24), kind=kOutput, calls=%fused_computation.27 | convolution fusion | flops 37748736 | bytes 12649216 | tf_op jit(solution)/shard_map/dot_general | solution.py:28
  437.0 5.7 %psum.47 = f32[192]{0:T(256)S(1)} all-reduce(f32[192]{0:T(256)S(1)} %bitcast.34), channel_id=1, replica_groups=mesh['rows'=8,'protos'=4] {'protos'}, use_global_device_ids=true, to_apply=%region_7.8 | all-reduce | flops 192 | bytes 1536 | tf_op jit(solution)/shard_map/psum | solution.py:29
  442.7 8.8 %multiply_convert_fusion = bf16[192,16384]{1,0:T(8,128)(2,1)} fusion(f32[192,16384]{1,0:T(8,128)} %copy-done, f32[16384]{0:T(1024)S(1)} %multiply_divide_fusion, f32[192]{0:T(256)S(1)} %divide_multiply_fusion), kind=kLoop, calls=%fused_computation.6 | loop fusion | flops 9437184 | bytes 18940672 | tf_op jit(solution)/shard_map/convert_element_type | solution.py:31
  (11 shorter events, 0.1 us)
Async XLA Ops:
  6.5 130.2 %all-gather.2.cloned.1.call-start = ((), (), s32[]{:S(2)}) async-start(), calls=%async_computation | async-start | bytes 9437184 | tf_op jit(solution)/shard_map/all_gather | solution.py:16
  7.3 219.2 %all-reduce.4.cloned.1.call-start = ((), (), s32[]{:S(2)}) async-start(), calls=%async_computation.1 | async-start | bytes 131072 | tf_op jit(solution)/shard_map/psum | solution.py:27
  147.7 4.6 copy-start
  158.9 166.0 %all-reduce.6.cloned.1.call-start = ((), (), s32[]{:S(2)}) async-start(), calls=%async_computation.2 | async-start | bytes 131072 | tf_op jit(solution)/shard_map/psum | solution.py:27
  255.2 168.3 %all-reduce.8.cloned.1.call-start = ((), (), s32[]{:S(2)}) async-start(), calls=%async_computation.3 | async-start | bytes 131072 | tf_op jit(solution)/shard_map/psum | solution.py:27
Sparse Core Ops, SparseCore 0:
  9.5 127.1 all-gather.1
  159.0 67.3 all-reduce.3
  255.3 69.4 all-reduce.5
  354.0 69.4 all-reduce.7
where the time goes:
time: 459 us; the launch traced here: 458 us
  waiting for transfers between devices  327 us (71%)
  matrix products  69.6 us (15%)
  blocking collectives  23.7 us (5%)
  other arithmetic  18.1 us (4%)
  between operations  13.2 us (3%)
  local copies, waits for them, and re-layouts  6.35 us (1%)
    psum x3, waiting for transfers between devices, on_device(): col_scale = 1.0 / (K * lax.psum(col_part, 'rows'))  207 us
    all_gather x1, waiting for transfers between devices, on_device(): full = lax.all_gather(prototypes, 'rows', axis=1, tiled=True)  120 us
    dot_general x3, matrix products, on_device(): row_part = jnp.dot(weights, col_scale, precision=lax.Precision.HIGHEST)  38.2 us
    dot_general x3, matrix products, on_device(): col_part = jnp.dot(row_scale, weights, precision=lax.Precision.HIGHEST)  25.6 us
    psum x3, blocking collectives, on_device(): row_scale = 1.0 / (total_rows * lax.psum(row_part, 'protos'))  17.2 us
  transfers between devices with their start and end apart: 4, of which 4 were waited for; matrix products, arithmetic and copies ran while one was open for 1% of the time, Pallas kernels for 0%

commit v1 on v0

--- a/solution.py
+++ b/solution.py
@@ -24,7 +24,7 @@
     row_scale = jnp.ones((patches.shape[0],), jnp.float32)
     for step in range(ITERS):
         col_part = jnp.dot(row_scale, weights, precision=lax.Precision.HIGHEST)
-        col_scale = 1.0 / (K * lax.psum(col_part, "rows"))
+        col_scale = 1.0 / (K * jnp.sum(lax.all_gather(col_part, "rows"), axis=0))
         row_part = jnp.dot(weights, col_scale, precision=lax.Precision.HIGHEST)
         row_scale = 1.0 / (total_rows * lax.psum(row_part, "protos"))
     factor = float(K) * float(total_rows)

time: 459 us -> 344 us (0.75)
  waiting for transfers between devices: 327 us -> 120 us
  blocking collectives: 23.7 us -> 119 us
    psum x3 -> x0, waiting for transfers between devices: 207 us -> none  [on_device(): col_scale = 1.0 / (K * lax.psum(col_part, 'rows'))]
    all_gather x0 -> x3, blocking collectives: none -> 95.4 us  [on_device(): col_scale = 1.0 / (K * jnp.sum(lax.all_gather(col_part, 'rows'), axis=0))]
  transfers between devices with their start and end apart: 4 -> 1, of which waited for: 4 -> 1; matrix products, arithmetic and copies ran while one was open for 1% -> 1% of each run, Pallas kernels for 0% -> 0%
where the time goes in v1:
time: 344 us; the launch traced here: 343 us
  waiting for transfers between devices  120 us (35%)
  blocking collectives  119 us (35%)
  matrix products  67.7 us (20%)
  other arithmetic  16 us (5%)
  between operations  13.5 us (4%)
  local copies, waits for them, and re-layouts  6.64 us (2%)
    all_gather x1, waiting for transfers between devices, on_device(): full = lax.all_gather(prototypes, 'rows', axis=1, tiled=True)  120 us
    all_gather x3, blocking collectives, on_device(): col_scale = 1.0 / (K * jnp.sum(lax.all_gather(col_part, 'rows'), axis=0))  95.4 us
    dot_general x3, matrix products, on_device(): row_part = jnp.dot(weights, col_scale, precision=lax.Precision.HIGHEST)  38.2 us
    dot_general x3, matrix products, on_device(): col_part = jnp.dot(row_scale, weights, precision=lax.Precision.HIGHEST)  23.8 us
    psum x3, blocking collectives, on_device(): row_scale = 1.0 / (total_rows * lax.psum(row_part, 'protos'))  17.3 us
    convert_element_type x1, other arithmetic, on_device(): (factor * row_scale[:, None] * weights * col_scale[None, :]).astype(jnp.b...  8.83 us
  transfers between devices with their start and end apart: 1, of which 1 were waited for; matrix products, arithmetic and copies ran while one was open for 1% of the time, Pallas kernels for 0%

profile of v1, /device:TPU:0, one launch (start us, length us, event | category | flops | bytes accessed | tf_op | source)
XLA Modules:
  0.0 343.4 jit_solution(13149025408473525254)
XLA Ops:
  6.5 0.7 all-gather.5.cloned.1.call-update
  7.3 0.9 copy.7
  8.2 0.7 compare_select_fusion
  8.9 0.8 gather_fusion
  9.7 0.7 compare_and_fusion
  10.3 0.1 broadcast_select_fusion
  10.4 0.1 copy.8
  10.5 6.5 %all_gather.24 = bf16[192,256]{0,1:T(8,128)(2,1)S(1)} all-gather(bf16[192,64]{0,1:T(8,128)(2,1)S(1)} %copy.8), channel_id=1, replica_groups=mesh['rows'=8,'protos'=4] {'protos'}, dimensions={1}, use_global_device_ids=true | all-gather | bytes 122880 | tf_op jit(solution)/shard_map/all_gather | solution.py:14
  17.0 0.1 multiply_reduce_fusion.1
  17.1 119.6 %all-gather.5.cloned.1.call-done = bf16[16384,256]{0,1:T(8,128)(2,1)} async-done(((bf16[16384,32]{0,1:T(8,128)(2,1)}), bf16[16384,256]{0,1:T(8,128)(2,1)}) %all-gather.5.cloned.1.call-update) | async-done | bytes 8388624 | tf_op jit(solution)/shard_map/all_gather | solution.py:16
  136.7 5.1 %multiply_reduce_fusion = f32[16384]{0:T(1024)S(1)} fusion(bf16[16384,256]{0,1:T(8,128)(2,1)} %all-gather.5.cloned.1.call-done), kind=kLoop, calls=%fused_computation.5 | loop fusion | flops 12566528 | bytes 8454144 | tf_op jit(solution)/shard_map/reduce_sum | solution.py:17
  141.8 5.8 %fusion.2 = f32[192,16384]{1,0:T(8,128)S(1)} fusion(bf16[192,256]{0,1:T(8,128)(2,1)S(1)} %all_gather.24, bf16[16384,256]{0,1:T(8,128)(2,1)} %all-gather.5.cloned.1.call-done, f32[16384]{0:T(1024)S(1)} %add_rsqrt_fusion, f32[192]{0:T(256)S(1)} %add_rsqrt_fusion.1), kind=kOutput, calls=%fused_computation.4 | convolution fusion | flops 1620049920 | bytes 21136128 | tf_op jit(solution)/shard_map/dot_general | solution.py:18
  147.7 4.6 %copy-done = f32[192,16384]{1,0:T(8,128)} copy-done((f32[192,16384]{1,0:T(8,128)}, f32[192,16384]{1,0:T(8,128)S(1)}, u32[]{:S(2)}) %copy-start) | copy-done | bytes 12582936
  152.2 6.0 %fusion.3 = f32[1,16384]{1,0:T(1,128)S(1)} fusion(f32[192,16384]{1,0:T(8,128)S(1)} %fusion.2), kind=kOutput, calls=%fused_computation.20 | convolution fusion | flops 37748736 | bytes 12648448 | tf_op jit(solution)/shard_map/dot_general | solution.py:26
  158.2 31.8 %all-gather = f32[131072]{0:T(1024)S(1)} all-gather(f32[16384]{0:T(1024)S(1)} %bitcast.27), channel_id=2, replica_groups=mesh['rows'=8,'protos'=4] {'rows'}, dimensions={0}, use_global_device_ids=true | all-gather | bytes 589824 | tf_op jit(solution)/shard_map/all_gather | solution.py:27
  190.0 0.1 reshape.27
  190.1 0.1 reduce_sum.47
  190.2 12.7 %fusion.6 = f32[1,192]{1,0:T(1,128)S(1)} fusion(f32[192,16384]{1,0:T(8,128)} %copy-done, f32[16384,1]{0,1:T(1,128)S(1)} %bitcast.28), kind=kOutput, calls=%fused_computation.23 | convolution fusion | flops 37748736 | bytes 12649216 | tf_op jit(solution)/shard_map/dot_general | solution.py:28
  203.0 5.7 %psum.21 = f32[192]{0:T(256)S(1)} all-reduce(f32[192]{0:T(256)S(1)} %bitcast.30), channel_id=1, replica_groups=mesh['rows'=8,'protos'=4] {'protos'}, use_global_device_ids=true, to_apply=%region_3.4 | all-reduce | flops 192 | bytes 1536 | tf_op jit(solution)/shard_map/psum | solution.py:29
  208.6 8.9 %fusion.7 = f32[1,16384]{1,0:T(1,128)S(1)} fusion(f32[192,1]{0,1:T(1,128)S(1)} %bitcast.31, f32[192,16384]{1,0:T(8,128)} %copy-done), kind=kOutput, calls=%fused_computation.24 | convolution fusion | flops 37748736 | bytes 12649216 | tf_op jit(solution)/shard_map/dot_general | solution.py:26
  217.5 31.8 %all-gather.1 = f32[131072]{0:T(1024)S(1)} all-gather(f32[16384]{0:T(1024)S(1)} %bitcast.25), channel_id=3, replica_groups=mesh['rows'=8,'protos'=4] {'rows'}, dimensions={0}, use_global_device_ids=true | all-gather | bytes 589824 | tf_op jit(solution)/shard_map/all_gather | solution.py:27
  249.3 0.1 reshape.28
  249.4 0.1 reduce_sum.48
  249.6 12.7 %fusion.8 = f32[1,192]{1,0:T(1,128)S(1)} fusion(f32[192,16384]{1,0:T(8,128)} %copy-done, f32[16384,1]{0,1:T(1,128)S(1)} %bitcast.29), kind=kOutput, calls=%fused_computation.25 | convolution fusion | flops 37748736 | bytes 12649216 | tf_op jit(solution)/shard_map/dot_general | solution.py:28
  262.3 5.7 %psum.22 = f32[192]{0:T(256)S(1)} all-reduce(f32[192]{0:T(256)S(1)} %bitcast.32), channel_id=1, replica_groups=mesh['rows'=8,'protos'=4] {'protos'}, use_global_device_ids=true, to_apply=%region_5.6 | all-reduce | flops 192 | bytes 1536 | tf_op jit(solution)/shard_map/psum | solution.py:29
  268.0 8.9 %fusion.9 = f32[1,16384]{1,0:T(1,128)S(1)} fusion(f32[192,1]{0,1:T(1,128)S(1)} %bitcast.33, f32[192,16384]{1,0:T(8,128)} %copy-done), kind=kOutput, calls=%fused_computation.26 | convolution fusion | flops 37748736 | bytes 12649216 | tf_op jit(solution)/shard_map/dot_general | solution.py:26
  276.9 31.8 %all-gather.2 = f32[131072]{0:T(1024)S(1)} all-gather(f32[16384]{0:T(1024)S(1)} %bitcast.26), channel_id=4, replica_groups=mesh['rows'=8,'protos'=4] {'rows'}, dimensions={0}, use_global_device_ids=true | all-gather | bytes 589824 | tf_op jit(solution)/shard_map/all_gather | solution.py:27
  308.7 0.1 reshape.29
  308.8 0.1 reduce_sum.49
  309.0 12.7 %fusion.10 = f32[1,192]{1,0:T(1,128)S(1)} fusion(f32[192,16384]{1,0:T(8,128)} %copy-done, f32[16384,1]{0,1:T(1,128)S(1)} %bitcast.24), kind=kOutput, calls=%fused_computation.27 | convolution fusion | flops 37748736 | bytes 12649216 | tf_op jit(solution)/shard_map/dot_general | solution.py:28
  321.7 6.0 %psum.23 = f32[192]{0:T(256)S(1)} all-reduce(f32[192]{0:T(256)S(1)} %bitcast.34), channel_id=1, replica_groups=mesh['rows'=8,'protos'=4] {'protos'}, use_global_device_ids=true, to_apply=%region_7.8 | all-reduce | flops 192 | bytes 1536 | tf_op jit(solution)/shard_map/psum | solution.py:29
  327.7 8.8 %multiply_convert_fusion = bf16[192,16384]{1,0:T(8,128)(2,1)} fusion(f32[192,16384]{1,0:T(8,128)} %copy-done, f32[16384]{0:T(1024)S(1)} %multiply_divide_fusion, f32[192]{0:T(256)S(1)} %divide_multiply_fusion), kind=kLoop, calls=%fused_computation.6 | loop fusion | flops 9437184 | bytes 18940672 | tf_op jit(solution)/shard_map/convert_element_type | solution.py:31
  (11 shorter events, 0.1 us)
Async XLA Ops:
  6.5 130.2 %all-gather.5.cloned.1.call-start = ((), (), s32[]{:S(2)}) async-start(), calls=%async_computation | async-start | bytes 9437184 | tf_op jit(solution)/shard_map/all_gather | solution.py:16
  147.7 4.6 %copy-start = (f32[192,16384]{1,0:T(8,128)}, f32[192,16384]{1,0:T(8,128)S(1)}, u32[]{:S(2)}) copy-start(f32[192,16384]{1,0:T(8,128)S(1)} %fusion.2) | copy-start | bytes 37748740
Sparse Core Ops, SparseCore 0:
  9.5 127.1 all-gather.4
